TPU v7x, 512 devices: a whole 4x8x8 slice. The times are simulated.
512 devices in a mesh: pipe: 2 (over core), tensor: 8 (over x, y_hi), expert: 32 (over y_lo, z).
Axes of the slice: x: 4, y: 8 (y_hi: 2, y_lo: 4; y = y_hi * 4 + y_lo), z: 8, core: 2. Of those that a mesh axis runs over, the one named last changes fastest.
Arguments:
- tokens: bfloat16 [3, 1536, 4096], P(None, 'expert', 'tensor'), may hold values from -36 to 36
- norm_gain: float32 [2, 4096], P('pipe'), may hold values from 0.1 to 1.9
- shared_gate: bfloat16 [2, 4096, 1024], P('pipe', 'expert', 'tensor'), may hold values from -0.09375 to 0.09375
- shared_up: bfloat16 [2, 4096, 1024], P('pipe', 'expert', 'tensor'), may hold values from -0.09375 to 0.09375
- shared_down: bfloat16 [2, 1024, 4096], P('pipe', 'tensor', 'expert'), may hold values from -0.1875 to 0.1875
- expert_gate: bfloat16 [2, 32, 4096, 1024], P('pipe', 'expert', None, 'tensor'), may hold values from -0.09375 to 0.09375
- expert_up: bfloat16 [2, 32, 4096, 1024], P('pipe', 'expert', None, 'tensor'), may hold values from -0.09375 to 0.09375
- expert_down: bfloat16 [2, 32, 1024, 4096], P('pipe', 'expert', 'tensor'), may hold values from -0.1875 to 0.1875
- expert_ids: int32 [2, 3, 1536, 8], P('pipe', None, 'expert'), may hold values from 0 to 255, as said below
- expert_slots: int32 [2, 3, 1536, 8], P('pipe', None, 'expert'), may hold values from -1 to 2, as said below
- route_weights: float32 [2, 3, 1536, 8], P('pipe', None, 'expert'), may hold values from 0.1 to 1
Outputs:
- states: bfloat16 [2, 3, 1536, 4096], P('pipe', None, 'expert', 'tensor')
Inputs may be any that keep to these rules, and one draw needn't show every extreme that they name: `expert_ids`: the 8 ids of a token are distinct. Ids of 32 and above name experts that are not held and add nothing. `expert_slots`: for a choice whose id is below 32: the number of earlier choices (earlier tokens, or lower k of the same token) of the same block of 48 tokens, same layer and microbatch, that name the same expert, if that number is below 3; otherwise -1. For ids of 32 and above: -1.
All inputs are finite; a program needn't handle non-finite values.
Results may differ from a plain program's by a relative error of at most 0.0085.
Values may be sent and summed in bfloat16 or wider, within the bound.
No kernel may reach another device: no remote copies, remote signals or barrier semaphores. Data moves between devices by JAX's collectives and lax.ppermute only.
A program may use at most 64 MiB of HBM per device.

v0:
```python
import jax
import jax.numpy as jnp
from jax import lax
from jax.sharding import PartitionSpec as P

CAP = 3


def turned_gather(arrays, axis, dims):
    turned = [jnp.moveaxis(a, dim, 0) for a, dim in zip(arrays, dims)]
    both = jnp.concatenate([t.reshape(len(t), -1) for t in turned], axis=1)
    filled, at, outs = (lax.all_gather(both, axis, axis=0, tiled=True), 0, [])
    for t, dim in zip(turned, dims):
        share = filled[:, at : at + t[0].size].reshape(-1, *t.shape[1:])
        outs.append(jnp.moveaxis(share, 0, dim))
        at += t[0].size
    return tuple(outs)


def laid_out(blocks, dim):
    shape = list(blocks.shape[1:])
    shape[dim] *= blocks.shape[0]
    return jnp.moveaxis(blocks, 0, dim).reshape(shape)


def from_everyone(x, axis):
    copies = jnp.broadcast_to(x, (lax.axis_size(axis), *x.shape))
    return lax.all_to_all(copies, axis, split_axis=0, concat_axis=0, tiled=True)


def gather_directly(x, axis, dim):
    return laid_out(from_everyone(x, axis), dim)


def in_blocks(x, dim, peers):
    shape = x.shape
    blocks = x.reshape(*shape[:dim], peers, shape[dim] // peers, *shape[dim + 1 :])
    return jnp.moveaxis(blocks, dim, 0)


def sent_and_summed(x, axis, dim):
    blocks = in_blocks(x, dim, lax.axis_size(axis))
    arrived = lax.all_to_all(blocks, axis, split_axis=0, concat_axis=0, tiled=True)
    return arrived.astype(jnp.float32).sum(axis=0)


def from_behind(value, axis, steps):
    count = lax.axis_size(axis)
    initial, last = (max(0, -steps), min(count, count - steps))
    return lax.ppermute(value, axis, [(source, source + steps) for source in range(initial, last)])


def product(left, right):
    return jnp.dot(left, right, preferred_element_type=jnp.float32)


def per_device(
    tokens,
    norm_gain,
    shared_gate,
    shared_up,
    shared_down,
    expert_gate,
    expert_up,
    expert_down,
    expert_ids,
    expert_slots,
    route_weights,
):
    section_index = lax.axis_index("pipe")
    n_experts = lax.axis_size("expert")
    n_tensor = lax.axis_size("tensor")
    batches = tokens.shape[0]
    shard_rows = tokens.shape[1]
    slice_width = tokens.shape[2]
    model_width = slice_width * n_tensor
    capacity = CAP
    slot_total = n_experts * capacity
    slot_range = jnp.arange(slot_total, dtype=jnp.int32)
    shared_gate_full, shared_up_full, shared_down_full = turned_gather(
        (shared_gate[0], shared_up[0], shared_down[0]), "expert", (0, 0, 1)
    )
    local_gate = expert_gate[0, 0]
    local_up = expert_up[0, 0]
    local_down = expert_down[0, 0]
    layer_gain = norm_gain[0]
    incoming = jnp.zeros((shard_rows, slice_width), jnp.bfloat16)
    produced = []
    for step_index in range(batches + 1):
        fresh_rows = tokens[min(step_index, batches - 1)]
        current = jnp.where(section_index == 0, fresh_rows, incoming)
        batch_index = jnp.clip(step_index - section_index, 0, batches - 1)
        route_ids = lax.dynamic_index_in_dim(expert_ids[0], batch_index, 0, keepdims=False)
        slot_rank = lax.dynamic_index_in_dim(expert_slots[0], batch_index, 0, keepdims=False)
        weights = lax.dynamic_index_in_dim(route_weights[0], batch_index, 0, keepdims=False)
        full_rows = gather_directly(current, "tensor", 1)
        values = full_rows.astype(jnp.float32)
        inverse_rms = lax.rsqrt(jnp.mean(values * values, axis=-1, keepdims=True) + 1e-06)
        normed = (values * inverse_rms * layer_gain).astype(jnp.bfloat16)
        shared_hidden = (
            jax.nn.silu(product(normed, shared_gate_full)) * product(normed, shared_up_full)
        ).astype(jnp.bfloat16)
        partial_value = product(shared_hidden, shared_down_full)
        valid = (route_ids < n_experts) & (slot_rank >= 0)
        slot_code = jnp.where(valid, route_ids * capacity + slot_rank, -1)
        matched = slot_code[:, :, None] == slot_range[None, None, :]
        picker = jnp.any(matched, axis=1).T.astype(jnp.bfloat16)
        combine = jnp.sum(jnp.where(matched, weights[:, :, None], jnp.float32(0.0)), axis=1)
        outgoing = (
            product(picker, normed).astype(jnp.bfloat16).reshape(n_experts, capacity, model_width)
        )
        arrived = lax.all_to_all(
            outgoing, "expert", split_axis=0, concat_axis=0, tiled=True
        ).reshape(slot_total, model_width)
        gate_rows = product(arrived, local_gate)
        up_rows = product(arrived, local_up)
        expert_hidden = (jax.nn.silu(gate_rows) * up_rows).astype(jnp.bfloat16)
        outcome = (
            product(expert_hidden, local_down)
            .astype(jnp.bfloat16)
            .reshape(n_experts, capacity, model_width)
        )
        returned = lax.all_to_all(
            outcome, "expert", split_axis=0, concat_axis=0, tiled=True
        ).reshape(slot_total, model_width)
        routed = jnp.dot(combine, returned.astype(jnp.float32), preferred_element_type=jnp.float32)
        summed = sent_and_summed((partial_value + routed).astype(jnp.bfloat16), "tensor", 1)
        result = (current.astype(jnp.float32) + summed).astype(jnp.bfloat16)
        produced.append(result)
        if step_index < batches:
            incoming = from_behind(result, "pipe", 1)
    outputs = [
        jnp.where(section_index == 0, produced[index_now], produced[index_now + 1])
        for index_now in range(batches)
    ]
    return jnp.stack(outputs)[None]


def solution(mesh):
    in_specs = (
        P(None, "expert", "tensor"),
        P("pipe", None),
        P("pipe", "expert", "tensor"),
        P("pipe", "expert", "tensor"),
        P("pipe", "tensor", "expert"),
        P("pipe", "expert", None, "tensor"),
        P("pipe", "expert", None, "tensor"),
        P("pipe", "expert", "tensor", None),
        P("pipe", None, "expert", None),
        P("pipe", None, "expert", None),
        P("pipe", None, "expert", None),
    )
    out_specs = P("pipe", None, "expert", "tensor")
    return jax.shard_map(
        per_device, mesh=mesh, in_specs=in_specs, out_specs=out_specs, check_vma=False
    )
```

profile of v0, /device:TPU:1, one launch (start us, length us, event | category | flops | bytes accessed | tf_op | source)
XLA Modules:
  0.0 610.0 jit_solution(16635909837770484328)
XLA Ops:
  8.2 10.1 %all-to-all-start = ((bf16[8,48,512]{2,1,0:T(8,128)(2,1)}), bf16[8,48,512]{2,1,0:T(8,128)(2,1)S(1)}, u32[]{:S(2)}, u32[]{:S(2)}) async-start(bf16[8,48,512]{2,1,0:T(8,128)(2,1)} %broadcast_in_dim.80), calls=%async_computation | async-start | bytes 786432 | tf_op jit(solution)/shard_map/all_to_all | solution.py:28
  23.2 7.0 %all-to-all-done = bf16[8,48,512]{2,1,0:T(8,128)(2,1)S(1)} async-done(((bf16[8,48,512]{2,1,0:T(8,128)(2,1)}), bf16[8,48,512]{2,1,0:T(8,128)(2,1)S(1)}, u32[]{:S(2)}, u32[]{:S(2)}) %all-to-all-start) | async-done | bytes 393248 | tf_op jit(solution)/shard_map/all_to_all | solution.py:28
  32.5 42.4 %all_to_all.80 = bf16[32,3,4096]{2,1,0:T(4,128)(2,1)} all-to-all(bf16[32,3,4096]{2,1,0:T(4,128)(2,1)} %reshape.259), channel_id=1, replica_groups=mesh['pipe'=2,'tensor'=8,'expert'=32] {'expert'}, dimensions={0} | all-to-all | bytes 1572864 | tf_op jit(solution)/shard_map/all_to_all | solution.py:112
  74.9 2.5 reshape.260
  77.4 2.1 fusion.34
  79.5 2.7 convolution_convert_fusion.3
  82.2 2.3 reshape.261
  84.5 8.6 %all-to-all-start.2 = ((bf16[32,3,4096]{2,1,0:T(4,128)(2,1)}), bf16[32,3,4096]{2,1,0:T(4,128)(2,1)}, u32[]{:S(2)}, u32[]{:S(2)}) async-start(bf16[32,3,4096]{2,1,0:T(4,128)(2,1)} %reshape.261), calls=%async_computation.2 | async-start | bytes 2097152 | tf_op jit(solution)/shard_map/all_to_all | solution.py:123
  95.8 1.5 select_reduce_fusion.3
  97.4 23.6 %all-to-all-done.2 = bf16[32,3,4096]{2,1,0:T(4,128)(2,1)} async-done(((bf16[32,3,4096]{2,1,0:T(4,128)(2,1)}), bf16[32,3,4096]{2,1,0:T(4,128)(2,1)}, u32[]{:S(2)}, u32[]{:S(2)}) %all-to-all-start.2) | async-done | bytes 786464 | tf_op jit(solution)/shard_map/all_to_all | solution.py:123
  121.0 2.5 reshape.262
  123.4 56.3 %all-gather.2.cloned.1.call-done = bf16[4096,384]{0,1:T(8,128)(2,1)} async-done(((bf16[128,384]{0,1:T(8,128)(2,1)}), bf16[4096,384]{0,1:T(8,128)(2,1)}) %all-gather.2.cloned.1.call-update) | async-done | bytes 3145744 | tf_op jit(solution)/shard_map/all_gather | solution.py:12
  179.7 2.3 fusion.58
  182.0 3.4 fusion.15
  185.4 1.7 fusion
  187.1 19.5 %all_to_all.81 = bf16[8,48,512]{2,1,0:T(8,128)(2,1)S(1)} all-to-all(bf16[8,48,512]{2,1,0:T(8,128)(2,1)S(1)} %bitcast.150), channel_id=1, replica_groups=mesh['pipe'=2,'tensor'=8,'expert'=32] {'tensor'}, dimensions={0} | all-to-all | bytes 786432 | tf_op jit(solution)/shard_map/all_to_all | solution.py:43
  208.0 21.5 %collective-permute-done = bf16[48,512]{1,0:T(8,128)(2,1)S(1)} collective-permute-done((bf16[48,512]{1,0:T(8,128)(2,1)S(1)}, bf16[48,512]{1,0:T(8,128)(2,1)S(1)}, u32[]{:S(2)}, u32[]{:S(2)}) %collective-permute-start) | collective-permute-done | bytes 49184 | tf_op jit(solution)/shard_map/ppermute | solution.py:50
  230.9 3.5 all-to-all-start.4
  235.7 1.5 fusion.62
  237.2 9.4 %all-to-all-done.4 = bf16[8,48,512]{2,1,0:T(8,128)(2,1)S(1)} async-done(((bf16[8,48,512]{2,1,0:T(8,128)(2,1)}), bf16[8,48,512]{2,1,0:T(8,128)(2,1)S(1)}, u32[]{:S(2)}, u32[]{:S(2)}) %all-to-all-start.4) | async-done | bytes 393248 | tf_op jit(solution)/shard_map/all_to_all | solution.py:28
  248.6 2.3 reshape.264
  250.9 35.8 %all_to_all.82 = bf16[32,3,4096]{2,1,0:T(4,128)(2,1)} all-to-all(bf16[32,3,4096]{2,1,0:T(4,128)(2,1)} %reshape.264), channel_id=1, replica_groups=mesh['pipe'=2,'tensor'=8,'expert'=32] {'expert'}, dimensions={0} | all-to-all | bytes 1572864 | tf_op jit(solution)/shard_map/all_to_all | solution.py:112
  286.6 2.5 reshape.265
  289.1 2.1 fusion.32
  291.2 2.8 convolution_convert_fusion.2
  294.0 2.3 reshape.266
  296.3 8.2 %all-to-all-start.6 = ((bf16[32,3,4096]{2,1,0:T(4,128)(2,1)}), bf16[32,3,4096]{2,1,0:T(4,128)(2,1)}, u32[]{:S(2)}, u32[]{:S(2)}) async-start(bf16[32,3,4096]{2,1,0:T(4,128)(2,1)} %reshape.266), calls=%async_computation.6 | async-start | bytes 2097152 | tf_op jit(solution)/shard_map/all_to_all | solution.py:123
  305.8 1.5 select_reduce_fusion.2
  307.3 2.3 fusion.56
  309.6 3.4 fusion.14
  313.0 17.1 %all-to-all-done.6 = bf16[32,3,4096]{2,1,0:T(4,128)(2,1)} async-done(((bf16[32,3,4096]{2,1,0:T(4,128)(2,1)}), bf16[32,3,4096]{2,1,0:T(4,128)(2,1)}, u32[]{:S(2)}, u32[]{:S(2)}) %all-to-all-start.6) | async-done | bytes 786464 | tf_op jit(solution)/shard_map/all_to_all | solution.py:123
  330.2 2.5 reshape.267
  332.6 1.6 fusion.1
  334.3 15.3 %all_to_all.83 = bf16[8,48,512]{2,1,0:T(8,128)(2,1)S(1)} all-to-all(bf16[8,48,512]{2,1,0:T(8,128)(2,1)S(1)} %bitcast.151), channel_id=1, replica_groups=mesh['pipe'=2,'tensor'=8,'expert'=32] {'tensor'}, dimensions={0} | all-to-all | bytes 786432 | tf_op jit(solution)/shard_map/all_to_all | solution.py:43
  351.6 4.9 collective-permute-done.1
  358.7 4.3 all-to-all-start.8
  365.8 9.5 %all-to-all-done.8 = bf16[8,48,512]{2,1,0:T(8,128)(2,1)S(1)} async-done(((bf16[8,48,512]{2,1,0:T(8,128)(2,1)}), bf16[8,48,512]{2,1,0:T(8,128)(2,1)S(1)}, u32[]{:S(2)}, u32[]{:S(2)}) %all-to-all-start.8) | async-done | bytes 393248 | tf_op jit(solution)/shard_map/all_to_all | solution.py:28
  377.3 2.3 reshape.269
  379.5 37.7 %all_to_all.84 = bf16[32,3,4096]{2,1,0:T(4,128)(2,1)} all-to-all(bf16[32,3,4096]{2,1,0:T(4,128)(2,1)} %reshape.269), channel_id=1, replica_groups=mesh['pipe'=2,'tensor'=8,'expert'=32] {'expert'}, dimensions={0} | all-to-all | bytes 1572864 | tf_op jit(solution)/shard_map/all_to_all | solution.py:112
  417.2 2.5 reshape.270
  419.7 2.1 fusion.30
  421.8 2.8 convolution_convert_fusion.1
  424.5 2.3 reshape.271
  426.8 7.7 %all-to-all-start.10 = ((bf16[32,3,4096]{2,1,0:T(4,128)(2,1)}), bf16[32,3,4096]{2,1,0:T(4,128)(2,1)}, u32[]{:S(2)}, u32[]{:S(2)}) async-start(bf16[32,3,4096]{2,1,0:T(4,128)(2,1)} %reshape.271), calls=%async_computation.10 | async-start | bytes 2097152 | tf_op jit(solution)/shard_map/all_to_all | solution.py:123
  435.9 1.5 select_reduce_fusion.1
  437.4 2.3 fusion.54
  439.7 3.4 fusion.13
  443.1 17.1 %all-to-all-done.10 = bf16[32,3,4096]{2,1,0:T(4,128)(2,1)} async-done(((bf16[32,3,4096]{2,1,0:T(4,128)(2,1)}), bf16[32,3,4096]{2,1,0:T(4,128)(2,1)}, u32[]{:S(2)}, u32[]{:S(2)}) %all-to-all-start.10) | async-done | bytes 786464 | tf_op jit(solution)/shard_map/all_to_all | solution.py:123
  460.2 2.5 reshape.272
  462.7 1.6 fusion.2
  464.3 13.3 %all_to_all.85 = bf16[8,48,512]{2,1,0:T(8,128)(2,1)S(1)} all-to-all(bf16[8,48,512]{2,1,0:T(8,128)(2,1)S(1)} %bitcast.152), channel_id=1, replica_groups=mesh['pipe'=2,'tensor'=8,'expert'=32] {'tensor'}, dimensions={0} | all-to-all | bytes 786432 | tf_op jit(solution)/shard_map/all_to_all | solution.py:43
  479.6 4.6 collective-permute-done.2
  486.5 4.5 all-to-all-start.12
  493.8 9.5 %all-to-all-done.12 = bf16[8,48,512]{2,1,0:T(8,128)(2,1)S(1)} async-done(((bf16[8,48,512]{2,1,0:T(8,128)(2,1)}), bf16[8,48,512]{2,1,0:T(8,128)(2,1)S(1)}, u32[]{:S(2)}, u32[]{:S(2)}) %all-to-all-start.12) | async-done | bytes 393248 | tf_op jit(solution)/shard_map/all_to_all | solution.py:28
  505.2 2.3 reshape.274
  507.5 38.0 %all_to_all.86 = bf16[32,3,4096]{2,1,0:T(4,128)(2,1)} all-to-all(bf16[32,3,4096]{2,1,0:T(4,128)(2,1)} %reshape.274), channel_id=1, replica_groups=mesh['pipe'=2,'tensor'=8,'expert'=32] {'expert'}, dimensions={0} | all-to-all | bytes 1572864 | tf_op jit(solution)/shard_map/all_to_all | solution.py:112
  545.5 2.5 reshape.275
  547.9 2.1 fusion.28
  550.0 1.8 convolution_convert_fusion
  553.2 8.0 %all-to-all-start.14 = ((bf16[32,3,4096]{2,1,0:T(4,128)(2,1)}), bf16[32,3,4096]{2,1,0:T(4,128)(2,1)S(1)}, u32[]{:S(2)}, u32[]{:S(2)}) async-start(bf16[32,3,4096]{2,1,0:T(4,128)(2,1)} %reshape.276), calls=%async_computation.14 | async-start | bytes 2097152 | tf_op jit(solution)/shard_map/all_to_all | solution.py:123
  561.5 1.7 fusion.52
  563.2 3.3 fusion.12
  566.6 20.4 %all-to-all-done.14 = bf16[32,3,4096]{2,1,0:T(4,128)(2,1)S(1)} async-done(((bf16[32,3,4096]{2,1,0:T(4,128)(2,1)}), bf16[32,3,4096]{2,1,0:T(4,128)(2,1)S(1)}, u32[]{:S(2)}, u32[]{:S(2)}) %all-to-all-start.14) | async-done | bytes 786464 | tf_op jit(solution)/shard_map/all_to_all | solution.py:123
  589.1 13.3 %all_to_all.87 = bf16[8,48,512]{2,1,0:T(8,128)(2,1)S(1)} all-to-all(bf16[8,48,512]{2,1,0:T(8,128)(2,1)S(1)} %bitcast.153), channel_id=1, replica_groups=mesh['pipe'=2,'tensor'=8,'expert'=32] {'tensor'}, dimensions={0} | all-to-all | bytes 786432 | tf_op jit(solution)/shard_map/all_to_all | solution.py:43
  (121 shorter events, 42.8 us)
Async XLA Ops:
  6.5 73.0 %copy-start = (bf16[1,1,128,4096]{3,2,1,0:T(8,128)(2,1)S(1)}, bf16[1,1,128,4096]{3,2,1,0:T(8,128)(2,1)}, u32[]{:S(2)}) copy-start(bf16[1,1,128,4096]{3,2,1,0:T(8,128)(2,1)} %param.18) | copy-start | bytes 3145732
  6.5 24.1 %copy-start.10 = (f32[1,4096]{1,0:T(1,128)S(1)}, f32[1,4096]{1,0:T(1,128)}, u32[]{:S(2)}) copy-start(f32[1,4096]{1,0:T(1,128)} %param.12) | copy-start | bytes 49156
  8.2 22.0 %all-to-all-start = ((bf16[8,48,512]{2,1,0:T(8,128)(2,1)}), bf16[8,48,512]{2,1,0:T(8,128)(2,1)S(1)}, u32[]{:S(2)}, u32[]{:S(2)}) async-start(bf16[8,48,512]{2,1,0:T(8,128)(2,1)} %broadcast_in_dim.80), calls=%async_computation | async-start | bytes 786432 | tf_op jit(solution)/shard_map/all_to_all | solution.py:28
  18.3 161.4 %all-gather.2.cloned.1.call-start = ((), (), s32[]{:S(2)}) async-start(), calls=%async_computation.16 | async-start | bytes 3244032 | tf_op jit(solution)/shard_map/all_gather | solution.py:12
  23.1 7.5 %copy-start.11 = (s32[48,8]{1,0:T(8,128)}, s32[48,8]{1,0:T(8,128)S(1)}, u32[]{:S(2)}) copy-start(s32[48,8]{1,0:T(8,128)S(1)} %copy.49) | copy-start | bytes 4612
  31.2 46.2 %copy-start.2 = (bf16[1,1,4096,128]{3,2,1,0:T(8,128)(2,1)S(1)}, bf16[1,1,4096,128]{3,2,1,0:T(8,128)(2,1)}, u32[]{:S(2)}) copy-start(bf16[1,1,4096,128]{3,2,1,0:T(8,128)(2,1)} %param.16) | copy-start | bytes 3145732
  32.5 47.0 %copy-start.1 = (bf16[1,1,4096,128]{3,2,1,0:T(8,128)(2,1)S(1)}, bf16[1,1,4096,128]{3,2,1,0:T(8,128)(2,1)}, u32[]{:S(2)}) copy-start(bf16[1,1,4096,128]{3,2,1,0:T(8,128)(2,1)} %param.17) | copy-start | bytes 3145732
  84.5 36.5 %all-to-all-start.2 = ((bf16[32,3,4096]{2,1,0:T(4,128)(2,1)}), bf16[32,3,4096]{2,1,0:T(4,128)(2,1)}, u32[]{:S(2)}, u32[]{:S(2)}) async-start(bf16[32,3,4096]{2,1,0:T(4,128)(2,1)} %reshape.261), calls=%async_computation.2 | async-start | bytes 2097152 | tf_op jit(solution)/shard_map/all_to_all | solution.py:123
  185.4 21.3 %copy-start.9 = (bf16[3,48,512]{2,1,0:T(8,128)(2,1)S(1)}, bf16[3,48,512]{2,1,0:T(8,128)(2,1)}, u32[]{:S(2)}) copy-start(bf16[3,48,512]{2,1,0:T(8,128)(2,1)} %param.11) | copy-start | bytes 442372
  206.7 22.8 %copy-start.17 = (bf16[48,512]{1,0:T(8,128)(2,1)}, bf16[48,512]{1,0:T(8,128)(2,1)S(1)}, u32[]{:S(2)}) copy-start(bf16[48,512]{1,0:T(8,128)(2,1)S(1)} %add_convert_fusion.3) | copy-start | bytes 147460
  206.7 22.8 %collective-permute-start = (bf16[48,512]{1,0:T(8,128)(2,1)S(1)}, bf16[48,512]{1,0:T(8,128)(2,1)S(1)}, u32[]{:S(2)}, u32[]{:S(2)}) collective-permute-start(bf16[48,512]{1,0:T(8,128)(2,1)S(1)} %add_convert_fusion.3), channel_id=1, source_target_pairs={{0,256},{1,257},{2,258},{3,259},{4,260},{5,261},{6,262},{7,263},{8... | collective-permute-start | bytes 147464 | tf_op jit(solution)/shard_map/ppermute | solution.py:50
  229.5 0.6 copy-start.3
  230.9 15.7 %all-to-all-start.4 = ((bf16[8,48,512]{2,1,0:T(8,128)(2,1)}), bf16[8,48,512]{2,1,0:T(8,128)(2,1)S(1)}, u32[]{:S(2)}, u32[]{:S(2)}) async-start(bf16[8,48,512]{2,1,0:T(8,128)(2,1)} %broadcast_in_dim.85), calls=%async_computation.4 | async-start | bytes 786432 | tf_op jit(solution)/shard_map/all_to_all | solution.py:28
  246.6 0.7 copy-start.21
  296.3 33.9 %all-to-all-start.6 = ((bf16[32,3,4096]{2,1,0:T(4,128)(2,1)}), bf16[32,3,4096]{2,1,0:T(4,128)(2,1)}, u32[]{:S(2)}, u32[]{:S(2)}) async-start(bf16[32,3,4096]{2,1,0:T(4,128)(2,1)} %reshape.266), calls=%async_computation.6 | async-start | bytes 2097152 | tf_op jit(solution)/shard_map/all_to_all | solution.py:123
  313.0 36.6 %copy-start.4 = (bf16[48,512]{1,0:T(8,128)(2,1)S(1)}, bf16[48,512]{1,0:T(8,128)(2,1)}, u32[]{:S(2)}) copy-start(bf16[48,512]{1,0:T(8,128)(2,1)} %copy-done.3) | copy-start | bytes 147460
  313.0 36.6 %copy-start.18 = (bf16[48,512]{1,0:T(8,128)(2,1)S(1)}, bf16[48,512]{1,0:T(8,128)(2,1)}, u32[]{:S(2)}) copy-start(bf16[48,512]{1,0:T(8,128)(2,1)} %copy-done.17) | copy-start | bytes 147460
  350.3 8.4 %copy-start.15 = (bf16[48,512]{1,0:T(8,128)(2,1)}, bf16[48,512]{1,0:T(8,128)(2,1)S(1)}, u32[]{:S(2)}) copy-start(bf16[48,512]{1,0:T(8,128)(2,1)S(1)} %get-tuple-element.6) | copy-start | bytes 147460
  350.3 6.1 %collective-permute-start.1 = (bf16[48,512]{1,0:T(8,128)(2,1)S(1)}, bf16[48,512]{1,0:T(8,128)(2,1)S(1)}, u32[]{:S(2)}, u32[]{:S(2)}) collective-permute-start(bf16[48,512]{1,0:T(8,128)(2,1)S(1)} %get-tuple-element.6), channel_id=1, source_target_pairs={{0,256},{1,257},{2,258},{3,259},{4,260},{5,261},{6,262},{7,263},{8... | collective-permute-start | bytes 147464 | tf_op jit(solution)/shard_map/ppermute | solution.py:50
  357.3 0.6 copy-start.5
  358.7 16.6 %all-to-all-start.8 = ((bf16[8,48,512]{2,1,0:T(8,128)(2,1)}), bf16[8,48,512]{2,1,0:T(8,128)(2,1)S(1)}, u32[]{:S(2)}, u32[]{:S(2)}) async-start(bf16[8,48,512]{2,1,0:T(8,128)(2,1)} %broadcast_in_dim.88), calls=%async_computation.8 | async-start | bytes 786432 | tf_op jit(solution)/shard_map/all_to_all | solution.py:28
  375.3 0.7 copy-start.22
  426.8 33.4 %all-to-all-start.10 = ((bf16[32,3,4096]{2,1,0:T(4,128)(2,1)}), bf16[32,3,4096]{2,1,0:T(4,128)(2,1)}, u32[]{:S(2)}, u32[]{:S(2)}) async-start(bf16[32,3,4096]{2,1,0:T(4,128)(2,1)} %reshape.271), calls=%async_computation.10 | async-start | bytes 2097152 | tf_op jit(solution)/shard_map/all_to_all | solution.py:123
  443.1 34.5 %copy-start.6 = (bf16[48,512]{1,0:T(8,128)(2,1)S(1)}, bf16[48,512]{1,0:T(8,128)(2,1)}, u32[]{:S(2)}) copy-start(bf16[48,512]{1,0:T(8,128)(2,1)} %copy-done.5) | copy-start | bytes 147460
  443.1 34.5 %copy-start.16 = (bf16[48,512]{1,0:T(8,128)(2,1)S(1)}, bf16[48,512]{1,0:T(8,128)(2,1)}, u32[]{:S(2)}) copy-start(bf16[48,512]{1,0:T(8,128)(2,1)} %copy-done.15) | copy-start | bytes 147460
  478.3 8.1 %copy-start.19 = (bf16[48,512]{1,0:T(8,128)(2,1)}, bf16[48,512]{1,0:T(8,128)(2,1)S(1)}, u32[]{:S(2)}) copy-start(bf16[48,512]{1,0:T(8,128)(2,1)S(1)} %get-tuple-element.8) | copy-start | bytes 147460
  478.3 5.9 collective-permute-start.2
  485.1 0.6 copy-start.7
  486.5 16.8 %all-to-all-start.12 = ((bf16[8,48,512]{2,1,0:T(8,128)(2,1)}), bf16[8,48,512]{2,1,0:T(8,128)(2,1)S(1)}, u32[]{:S(2)}, u32[]{:S(2)}) async-start(bf16[8,48,512]{2,1,0:T(8,128)(2,1)} %broadcast_in_dim.91), calls=%async_computation.12 | async-start | bytes 786432 | tf_op jit(solution)/shard_map/all_to_all | solution.py:28
  503.3 0.7 copy-start.23
  550.0 11.2 %copy-start.24 = (f32[48,8]{0,1:T(8,128)S(1)}, f32[48,8]{0,1:T(8,128)}, u32[]{:S(2)}) copy-start(f32[48,8]{0,1:T(8,128)} %get-tuple-element.13) | copy-start | bytes 4612
  550.0 11.3 %copy-start.12 = (s32[48,8]{1,0:T(8,128)S(1)}, s32[48,8]{1,0:T(8,128)}, u32[]{:S(2)}) copy-start(s32[48,8]{1,0:T(8,128)} %copy.61) | copy-start | bytes 4612
  553.2 33.8 %all-to-all-start.14 = ((bf16[32,3,4096]{2,1,0:T(4,128)(2,1)}), bf16[32,3,4096]{2,1,0:T(4,128)(2,1)S(1)}, u32[]{:S(2)}, u32[]{:S(2)}) async-start(bf16[32,3,4096]{2,1,0:T(4,128)(2,1)} %reshape.276), calls=%async_computation.14 | async-start | bytes 2097152 | tf_op jit(solution)/shard_map/all_to_all | solution.py:123
  566.5 35.9 %copy-start.8 = (bf16[48,512]{1,0:T(8,128)(2,1)S(1)}, bf16[48,512]{1,0:T(8,128)(2,1)}, u32[]{:S(2)}) copy-start(bf16[48,512]{1,0:T(8,128)(2,1)} %copy-done.7) | copy-start | bytes 147460
  566.5 35.9 %copy-start.20 = (bf16[48,512]{1,0:T(8,128)(2,1)S(1)}, bf16[48,512]{1,0:T(8,128)(2,1)}, u32[]{:S(2)}) copy-start(bf16[48,512]{1,0:T(8,128)(2,1)} %copy-done.19) | copy-start | bytes 147460
  566.5 35.9 %copy-start.13 = (bf16[1,48,512]{2,1,0:T(8,128)(2,1)S(1)}, bf16[1,48,512]{2,1,0:T(8,128)(2,1)}, u32[]{:S(2)}) copy-start(bf16[1,48,512]{2,1,0:T(8,128)(2,1)} %get-tuple-element.5) | copy-start | bytes 147460
  566.6 35.9 %copy-start.14 = (bf16[1,48,512]{2,1,0:T(8,128)(2,1)S(1)}, bf16[1,48,512]{2,1,0:T(8,128)(2,1)}, u32[]{:S(2)}) copy-start(bf16[1,48,512]{2,1,0:T(8,128)(2,1)} %get-tuple-element.7) | copy-start | bytes 147460
Sparse Core Ops, SparseCore 0:
  21.7 157.9 all-gather.1
where the time goes:
time: 619 us; the launch traced here: 610 us
  blocking collectives  215 us (35%)
  waiting for transfers between devices  201 us (32%)
  starting transfers between devices  58.7 us (9%)
  local copies, waits for them, and re-layouts  51.6 us (8%)
  matrix products  51.2 us (8%)
  other arithmetic  18.6 us (3%)
  between operations  13.9 us (2%)
    all_to_all x4, blocking collectives, per_device(): lax.all_to_all(outgoing, 'expert', split_axis=0, concat_axis=0, tiled=True)  154 us
    all_to_all x4, waiting for transfers between devices, per_device(): lax.all_to_all(outcome, 'expert', split_axis=0, concat_axis=0, tiled=True)  78.2 us
    all_to_all x4, blocking collectives, sent_and_summed(): lax.all_to_all(blocks, axis, split_axis=0, concat_axis=0, tiled=True)  61.3 us
    all_gather x1, waiting for transfers between devices, turned_gather(): filled, at, outs = (lax.all_gather(both, axis, axis=0, tiled=True), 0, [])  56.3 us
    dot_general x20, matrix products, product(): return jnp.dot(left, right, preferred_element_type=jnp.float32)  44.9 us
    all_to_all x4, waiting for transfers between devices, from_everyone(): return lax.all_to_all(copies, axis, split_axis=0, concat_axis=0, tiled=True)  35.4 us
    all_to_all x4, starting transfers between devices, per_device(): lax.all_to_all(outcome, 'expert', split_axis=0, concat_axis=0, tiled=True)  32.4 us
    ppermute x3, waiting for transfers between devices, from_behind(): lax.ppermute(value, axis, [(source, source + steps) for source in range(i...  31 us
  transfers between devices with their start and end apart: 12, of which 12 were waited for; matrix products, arithmetic and copies ran while one was open for 9% of the time, Pallas kernels for 0%

commit v1 on v0

v1 whole, which is shorter than its diff:
```python
import functools

import jax
import jax.numpy as jnp
from jax import lax
from jax.experimental import pallas as pl
from jax.experimental.pallas import tpu as pltpu
from jax.sharding import Mesh, PartitionSpec as P

CAP = 3
HELD = 32
SUB = ("pipe", "x", "yh", "yl", "z")
SWAP = [(0, 1), (1, 0)]
F32 = jnp.float32
BF16 = jnp.bfloat16


def to_all(v, axis):
    return lax.all_to_all(v, axis, split_axis=0, concat_axis=0, tiled=True)


def copies_to_all(v, axis):
    return to_all(jnp.broadcast_to(v, (lax.axis_size(axis), *v.shape)), axis)


def swapped(v):
    return lax.ppermute(v, "pipe", SWAP)


def normed_part(g_ref, gain_ref, inv, t):
    return (g_ref[t].astype(F32) * inv * gain_ref[pl.ds(t, 1), :]).astype(BF16)


def inverse_rms(g_ref):
    parts, rows, width = g_ref.shape
    total = jnp.zeros((rows, 1), F32)
    for t in range(parts):
        v = g_ref[t].astype(F32)
        total += jnp.sum(v * v, axis=-1, keepdims=True)
    return lax.rsqrt(total / (parts * width) + 1e-6)


def gated(gate, up):
    return (gate / (1.0 + jnp.exp(-gate)) * up).astype(BF16)


def take(first, ours, theirs, into, sems):
    for at, pair in enumerate((ours, theirs)):
        @pl.when(first == 1 - at)
        def _(pair=pair):
            for i, (src, dst) in enumerate(zip(pair, into)):
                pltpu.make_async_copy(src, dst, sems.at[i]).start()


def expert_kernel(first, g_ref, gain_ref, og, ou, od, tg, tu, td, out_ref, wg, wu, wd, sems):
    parts, rows, width = g_ref.shape
    take(first[0], (og, ou, od), (tg, tu, td), (wg, wu, wd), sems)
    inv = inverse_rms(g_ref)
    gate = jnp.zeros((rows, wg.shape[1]), F32)
    up = jnp.zeros((rows, wg.shape[1]), F32)
    pltpu.make_async_copy(og, wg, sems.at[0]).wait()
    pltpu.make_async_copy(ou, wu, sems.at[1]).wait()
    for t in range(parts):
        n = normed_part(g_ref, gain_ref, inv, t)
        gate += jnp.dot(n, wg[t * width : (t + 1) * width], preferred_element_type=F32)
        up += jnp.dot(n, wu[t * width : (t + 1) * width], preferred_element_type=F32)
    hidden = gated(gate, up)
    pltpu.make_async_copy(od, wd, sems.at[2]).wait()
    for t in range(parts):
        out_ref[t] = jnp.dot(
            hidden, wd[:, t * width : (t + 1) * width], preferred_element_type=F32
        ).astype(BF16)


def shared_kernel(first, g_ref, gain_ref, ow, tw, out_ref, w, sems):
    parts, rows, width = g_ref.shape
    n_z, n_yl, block, _ = w.shape
    take(first[0], (ow,), (tw,), (w,), sems)
    inv = inverse_rms(g_ref)
    both = jnp.zeros((rows, 2 * block), F32)
    pltpu.make_async_copy(ow, w, sems.at[0]).wait()
    per = width // block
    for t in range(parts):
        n = normed_part(g_ref, gain_ref, inv, t)
        for i in range(per):
            j = t * per + i
            both += jnp.dot(
                n[:, i * block : (i + 1) * block],
                w[j % n_z, j // n_z, :, : 2 * block],
                preferred_element_type=F32,
            )
    hidden = gated(both[:, :block], both[:, block:])
    for t in range(parts):
        for i in range(per):
            j = t * per + i
            out_ref[t, :, i * block : (i + 1) * block] = jnp.dot(
                hidden, w[j % n_z, j // n_z, :, 2 * block :], preferred_element_type=F32
            ).astype(BF16)


def call(kernel, first, g, gain, weights, scratch, name):
    vmem = pl.BlockSpec(memory_space=pltpu.VMEM)
    held = pl.BlockSpec(memory_space=pl.ANY)
    rows = g.shape[1]
    return pl.pallas_call(
        kernel,
        out_shape=jax.ShapeDtypeStruct(g.shape, BF16),
        in_specs=[pl.BlockSpec(memory_space=pltpu.SMEM), vmem, vmem] + [held] * len(weights),
        out_specs=vmem,
        scratch_shapes=[pltpu.VMEM(s, BF16) for s in scratch]
        + [pltpu.SemaphoreType.DMA((len(scratch),))],
        compiler_params=pltpu.CompilerParams(vmem_limit_bytes=32 * 2**20),
        cost_estimate=pl.CostEstimate(
            flops=6 * rows * 4096 * 128, bytes_accessed=4 * 2**20, transcendentals=rows * 128
        ),
        name=name,
    )(first, g, gain, *weights)


def per_device(
    tokens, norm_gain, shared_gate, shared_up, shared_down, expert_gate, expert_up, expert_down,
    expert_ids, expert_slots, route_weights,
):
    pipe = lax.axis_index("pipe")
    lower = pipe == 0
    batches, block, width = tokens.shape
    total = batches * block
    half = total // 2
    codes_of = 10
    mine = 5
    slots = HELD * mine
    n_tensor = lax.axis_size("x") * lax.axis_size("yh")

    ids, ranks = expert_ids[0], expert_slots[0]
    batch = lax.broadcasted_iota(jnp.int32, ids.shape, 0)
    valid = (ids < HELD) & (ranks >= 0)
    code = jnp.where(valid, ids * codes_of + batch * CAP + ranks, -1)
    table = jnp.concatenate([code.astype(F32), route_weights[0]], axis=-1).reshape(total, -1)
    table_there = swapped(table)
    gain = norm_gain[0].reshape(n_tensor, width)
    gain_there = swapped(gain)

    share = jnp.concatenate([shared_gate[0], shared_up[0], shared_down[0]], axis=1)
    share = copies_to_all(share, "yl")
    share = lax.all_gather(share, "z", axis=0)
    share_there = swapped(share)

    own = (expert_gate[0, 0], expert_up[0, 0], expert_down[0, 0])
    there = tuple(swapped(w) for w in own)

    slot = lax.broadcasted_iota(jnp.int32, (slots, 1, 1), 0)
    target = slot // mine * codes_of + slot % mine + mine * pipe
    target_f = target.astype(F32)

    state = tokens.reshape(total, width)
    produced = []
    for layer in range(2):
        here = pipe == layer
        first = here.astype(jnp.int32).reshape(1)
        routes = jnp.where(here, table, table_there)
        layer_gain = jnp.where(here, gain, gain_there)
        top = routes.shape[1] // 2
        route_code, route_weight = routes[:, :top], routes[:, top:]
        match = target_f == route_code[None]
        picker = jnp.any(match, axis=-1).astype(BF16)
        combine = jnp.sum(jnp.where(match, route_weight[None], 0.0), axis=-1)

        sent = jnp.dot(picker, state, preferred_element_type=F32).astype(BF16)
        sent = sent.reshape(HELD, mine, width // 128, 128)
        sent = jnp.broadcast_to(sent, (2, *sent.shape)).reshape(2 * HELD, mine, width // 128, 128)
        came = to_all(sent, ("yh", "yl", "z")).reshape(2, slots, width)
        rows = copies_to_all(came, "x").reshape(n_tensor, slots, width)
        parts = call(
            expert_kernel, first, rows, layer_gain, (*own, *there),
            [w.shape for w in own], "expert",
        )
        parts = to_all(parts.reshape(-1, 2 * slots, width), "x")
        parts = parts.astype(F32).sum(axis=0).astype(BF16)
        parts = parts.reshape(2 * HELD, mine, width // 128, 128)
        back = to_all(parts, ("yh", "yl", "z")).reshape(2, slots, width)
        back = back.astype(F32).sum(axis=0)
        routed = lax.dot_general(
            combine, back, (((0,), (0,)), ((), ())), preferred_element_type=F32
        )

        ours = jnp.where(lower, state[:half], state[half:])
        pair = copies_to_all(ours, "yh")
        full = copies_to_all(pair, "x").reshape(n_tensor, half, width)
        terms = call(
            shared_kernel, first, full, layer_gain, (share, share_there), [share.shape], "shared"
        )
        terms = to_all(terms.reshape(-1, 2 * half, width), "x")
        terms = terms.astype(F32).sum(axis=0).astype(BF16).reshape(2, half, width)
        terms = to_all(terms, "yh").astype(F32).sum(axis=0)
        none = jnp.zeros_like(terms)
        placed = jnp.concatenate(
            [jnp.where(lower, terms, none), jnp.where(lower, none, terms)], axis=0
        )
        added = (routed + placed).astype(BF16)
        added_there = swapped(added)
        state = (state.astype(F32) + (added.astype(F32) + added_there.astype(F32))).astype(BF16)
        produced.append(state)
    out = jnp.where(lower, produced[0], produced[1])
    return out.reshape(1, batches, block, width)


def solution(mesh):
    fine = Mesh(mesh.devices.reshape(2, 4, 2, 4, 8), SUB)
    tensor, expert = ("x", "yh"), ("yl", "z")
    in_specs = (
        P(None, expert, tensor),
        P("pipe", None),
        P("pipe", expert, tensor),
        P("pipe", expert, tensor),
        P("pipe", tensor, expert),
        P("pipe", expert, None, tensor),
        P("pipe", expert, None, tensor),
        P("pipe", expert, tensor, None),
        P("pipe", None, expert, None),
        P("pipe", None, expert, None),
        P("pipe", None, expert, None),
    )
    return jax.shard_map(
        per_device, mesh=fine, in_specs=in_specs, out_specs=P("pipe", None, expert, tensor),
        check_vma=False,
    )
```

time: 619 us -> 375 us (0.61); the launches traced: 610 us -> 373 us
  blocking collectives: 215 us -> 33.4 us
  starting transfers between devices: 58.7 us -> 124 us
  waiting for transfers between devices: 201 us -> 140 us
  matrix products: 51.2 us -> 1.53 us
  local copies, waits for them, and re-layouts: 51.6 us -> 30.8 us
  Pallas kernels: 0 us -> 15 us
    all_to_all x8 -> x2, blocking collectives: 215 us -> 33.4 us  [to_all(): return lax.all_to_all(v, axis, split_axis=0, concat_axis=0, tiled=True)]
    dot_general x24 -> x4, matrix products: 51.2 us -> 1.53 us  [the longest x2 1.18 us: per_device(): sent = jnp.dot(picker, state, preferred_element_type=F32).astype(BF16)]
    ppermute x3 -> x8, starting transfers between devices: 3.85 us -> 38.3 us  [swapped(): return lax.ppermute(v, 'pipe', SWAP)]
    all_to_all x8 -> x15, starting transfers between devices: 54.8 us -> 85.5 us  [to_all(): return lax.all_to_all(v, axis, split_axis=0, concat_axis=0, tiled=True)]
    reshape x20 -> x6, local copies, waits for them, and re-layouts: 34.3 us -> 6.27 us  [the longest x2 2.66 us: per_device(): parts = parts.reshape(2 * HELD, mine, width // 128, 128)]
    ppermute x3 -> x8, waiting for transfers between devices: 31 us -> 3.71 us  [swapped(): return lax.ppermute(v, 'pipe', SWAP)]
    all_gather x1, waiting for transfers between devices: 56.3 us -> 36.9 us  [per_device(): share = lax.all_gather(share, 'z', axis=0)]
    pallas_call x0 -> x4, Pallas kernels: none -> 15 us  [call(): pl.pallas_call(kernel, out_shape=jax.ShapeDtypeStruct(g.shape, BF16), in_...]
  transfers between devices with their start and end apart: 12 -> 24, of which waited for: 12 -> 18; matrix products, arithmetic and copies ran while one was open for 9% -> 7% of each run, Pallas kernels for 0% -> 4%
where the time goes in v1:
time: 375 us; the launch traced here: 373 us
  waiting for transfers between devices  140 us (37%)
  starting transfers between devices  124 us (33%)
  blocking collectives  33.4 us (9%)
  local copies, waits for them, and re-layouts  30.8 us (8%)
  Pallas kernels  15 us (4%)
  other arithmetic  14 us (4%)
  between operations  14 us (4%)
    all_to_all x15, waiting for transfers between devices, to_all(): return lax.all_to_all(v, axis, split_axis=0, concat_axis=0, tiled=True)  99.7 us
    all_to_all x15, starting transfers between devices, to_all(): return lax.all_to_all(v, axis, split_axis=0, concat_axis=0, tiled=True)  85.5 us
    ppermute x8, starting transfers between devices, swapped(): return lax.ppermute(v, 'pipe', SWAP)  38.3 us
    all_gather x1, waiting for transfers between devices, per_device(): share = lax.all_gather(share, 'z', axis=0)  36.9 us
    all_to_all x2, blocking collectives, to_all(): return lax.all_to_all(v, axis, split_axis=0, concat_axis=0, tiled=True)  33.4 us
    pallas_call x4, Pallas kernels, call(): pl.pallas_call(kernel, out_shape=jax.ShapeDtypeStruct(g.shape, BF16), in_...  15 us
    unnamed x57, local copies, waits for them, and re-layouts  10.8 us
    broadcast_in_dim x7, local copies, waits for them, and re-layouts, copies_to_all(): return to_all(jnp.broadcast_to(v, (lax.axis_size(axis), *v.shape)), axis)  8.43 us
  transfers between devices with their start and end apart: 24, of which 18 were waited for; matrix products, arithmetic and copies ran while one was open for 7% of the time, Pallas kernels for 4%

profile of v1, /device:TPU:1, one launch (start us, length us, event | category | flops | bytes accessed | tf_op | source)
XLA Modules:
  0.0 372.8 jit_solution(11005697029823649984)
XLA Ops:
  7.4 13.2 %all_to_all.85 = bf16[4,128,384]{2,1,0:T(8,128)(2,1)} all-to-all(bf16[4,128,384]{2,1,0:T(8,128)(2,1)S(1)} %broadcast_in_dim.60), channel_id=1, replica_groups=mesh['pipe'=2,'x'=4,'yh'=2,'yl'=4,'z'=8] {'yl'}, dimensions={0} | all-to-all | bytes 786432 | tf_op jit(solution)/shard_map/all_to_all | solution.py:19
  21.2 7.7 %collective-permute-start = (f32[144,16]{0,1:T(8,128)S(1)}, f32[144,16]{0,1:T(8,128)S(1)}, u32[]{:S(2)}, u32[]{:S(2)}) collective-permute-start(f32[144,16]{0,1:T(8,128)S(1)} %pad_maximum_fusion.1), channel_id=1, source_target_pairs={{0,256},{256,0},{1,257},{257,1},{2,258},{258,2},{3,259},{259,3},{4... | collective-permute-start | bytes 27656 | tf_op jit(solution)/shard_map/ppermute | solution.py:27
  32.5 14.0 %all-to-all-start = ((bf16[64,5,4,128]{3,2,1,0:T(4,128)(2,1)}), bf16[64,5,4,128]{3,2,1,0:T(4,128)(2,1)S(1)}, u32[]{:S(2)}, u32[]{:S(2)}) async-start(bf16[64,5,4,128]{3,2,1,0:T(4,128)(2,1)} %bitcast.2), calls=%async_computation | async-start | bytes 655360 | tf_op jit(solution)/shard_map/all_to_all | solution.py:19
  46.6 36.9 %all-gather.3.cloned.1.call-done = bf16[32,128,384]{2,1,0:T(8,128)(2,1)} async-done(((bf16[4,128,384]{2,1,0:T(8,128)(2,1)}), bf16[32,128,384]{2,1,0:T(8,128)(2,1)}) %all-gather.3.cloned.1.call-update) | async-done | bytes 3145744 | tf_op jit(solution)/shard_map/all_gather | solution.py:145
  83.5 2.7 collective-permute-start.5
  86.9 6.4 %all-to-all-start.4 = ((bf16[2,72,512]{2,1,0:T(8,128)(2,1)}), bf16[2,72,512]{2,1,0:T(8,128)(2,1)S(1)}, u32[]{:S(2)}, u32[]{:S(2)}) async-start(bf16[2,72,512]{2,1,0:T(8,128)(2,1)} %broadcast_in_dim.58), calls=%async_computation.4 | async-start | bytes 294912 | tf_op jit(solution)/shard_map/all_to_all | solution.py:19
  93.5 7.5 %all-to-all-done.4 = bf16[2,72,512]{2,1,0:T(8,128)(2,1)S(1)} async-done(((bf16[2,72,512]{2,1,0:T(8,128)(2,1)}), bf16[2,72,512]{2,1,0:T(8,128)(2,1)S(1)}, u32[]{:S(2)}, u32[]{:S(2)}) %all-to-all-start.4) | async-done | bytes 147488 | tf_op jit(solution)/shard_map/all_to_all | solution.py:19
  101.0 1.2 broadcast_in_dim.57
  102.2 4.1 %all-to-all-start.1 = ((bf16[4,2,160,512]{3,2,1,0:T(8,128)(2,1)}), bf16[4,2,160,512]{3,2,1,0:T(8,128)(2,1)S(1)}, u32[]{:S(2)}, u32[]{:S(2)}) async-start(bf16[4,2,160,512]{3,2,1,0:T(8,128)(2,1)} %broadcast_in_dim.57), calls=%async_computation.1 | async-start | bytes 2621440 | tf_op jit(solution)/shard_map/all_to_all | solution.py:19
  106.3 3.5 collective-permute-start.2
  109.8 1.9 collective-permute-start.3
  111.7 2.4 collective-permute-start.4
  114.1 8.7 %all-to-all-done.1 = bf16[4,2,160,512]{3,2,1,0:T(8,128)(2,1)S(1)} async-done(((bf16[4,2,160,512]{3,2,1,0:T(8,128)(2,1)}), bf16[4,2,160,512]{3,2,1,0:T(8,128)(2,1)S(1)}, u32[]{:S(2)}, u32[]{:S(2)}) %all-to-all-start.1) | async-done | bytes 1310752 | tf_op jit(solution)/shard_map/all_to_all | solution.py:19
  122.9 1.9 broadcast_in_dim.59
  124.8 4.1 %all-to-all-start.5 = ((bf16[4,2,72,512]{3,2,1,0:T(8,128)(2,1)}), bf16[4,2,72,512]{3,2,1,0:T(8,128)(2,1)}, u32[]{:S(2)}, u32[]{:S(2)}) async-start(bf16[4,2,72,512]{3,2,1,0:T(8,128)(2,1)} %broadcast_in_dim.59), calls=%async_computation.5 | async-start | bytes 1179648 | tf_op jit(solution)/shard_map/all_to_all | solution.py:19
  130.2 4.2 %collective-permute-start.1 = (f32[8,512]{1,0:T(8,128)S(1)}, f32[8,512]{1,0:T(8,128)}, u32[]{:S(2)}, u32[]{:S(2)}) collective-permute-start(f32[8,512]{1,0:T(8,128)S(1)} %reshape_squeeze.3), channel_id=1, source_target_pairs={{0,256},{256,0},{1,257},{257,1},{2,258},{258,2},{3,259},{259,3},{4... | collective-permute-start | bytes 49160 | tf_op jit(solution)/shard_map/ppermute | solution.py:27
  136.1 1.3 copy-done.2
  137.4 1.2 copy-done.5
  138.7 1.2 copy-done.8
  139.9 1.2 copy-done.10
  141.1 3.0 expert.2
  144.2 1.1 copy-done.3
  145.3 4.5 %all-to-all-start.2 = ((bf16[4,320,512]{2,1,0:T(8,128)(2,1)}), bf16[4,320,512]{2,1,0:T(8,128)(2,1)}, u32[]{:S(2)}, u32[]{:S(2)}) async-start(bf16[4,320,512]{2,1,0:T(8,128)(2,1)} %bitcast.44), calls=%async_computation.2 | async-start | bytes 2621440 | tf_op jit(solution)/shard_map/all_to_all | solution.py:19
  149.8 4.6 %shared.2 = bf16[8,72,512]{2,1,0:T(8,128)(2,1)S(1)} custom-call(s32[1]{0:T(128)} %bitcast.1.first, bf16[8,72,512]{2,1,0:T(8,128)(2,1)} %bitcast.8.g_ref, f32[8,512]{1,0:T(8,128)S(1)} %get-tuple-element.14.gain_ref, bf16[8,4,128,384]{3,2,1,0:T(8,128)(2,1)S(1)} %bitcast.41, bf16[8,4,128,384]{3,2,1,0:T(8,128)(2,1)} %collective-permute-done.5.tw), custom_call_target="tpu_custom_call" | custom-call | flops 226492416 | bytes 4194304 | tf_op jit(solution)/shard_map/shared/pallas_call | solution.py:105
  155.2 13.0 %all-to-all-done.2 = bf16[4,320,512]{2,1,0:T(8,128)(2,1)} async-done(((bf16[4,320,512]{2,1,0:T(8,128)(2,1)}), bf16[4,320,512]{2,1,0:T(8,128)(2,1)}, u32[]{:S(2)}, u32[]{:S(2)}) %all-to-all-start.2) | async-done | bytes 1310752 | tf_op jit(solution)/shard_map/all_to_all | solution.py:19
  168.2 4.2 %all-to-all-start.7 = ((bf16[4,144,512]{2,1,0:T(8,128)(2,1)}), bf16[4,144,512]{2,1,0:T(8,128)(2,1)}, u32[]{:S(2)}, u32[]{:S(2)}) async-start(bf16[4,144,512]{2,1,0:T(8,128)(2,1)} %bitcast.55), calls=%async_computation.7 | async-start | bytes 1179648 | tf_op jit(solution)/shard_map/all_to_all | solution.py:19
  172.4 2.3 reduce_sum.103
  174.7 1.8 reshape.141
  176.6 5.7 %all-to-all-done.7 = bf16[4,144,512]{2,1,0:T(8,128)(2,1)} async-done(((bf16[4,144,512]{2,1,0:T(8,128)(2,1)}), bf16[4,144,512]{2,1,0:T(8,128)(2,1)}, u32[]{:S(2)}, u32[]{:S(2)}) %all-to-all-start.7) | async-done | bytes 589856 | tf_op jit(solution)/shard_map/all_to_all | solution.py:19
  182.3 7.2 %all-to-all-start.3 = ((bf16[64,5,4,128]{3,2,1,0:T(4,128)(2,1)}), bf16[64,5,4,128]{3,2,1,0:T(4,128)(2,1)}, u32[]{:S(2)}, u32[]{:S(2)}) async-start(bf16[64,5,4,128]{3,2,1,0:T(4,128)(2,1)} %reshape.141), calls=%async_computation.3 | async-start | bytes 655360 | tf_op jit(solution)/shard_map/all_to_all | solution.py:19
  189.8 1.9 reduce_sum.105
  191.6 11.0 %all-to-all-done.3 = bf16[64,5,4,128]{3,2,1,0:T(4,128)(2,1)} async-done(((bf16[64,5,4,128]{3,2,1,0:T(4,128)(2,1)}), bf16[64,5,4,128]{3,2,1,0:T(4,128)(2,1)}, u32[]{:S(2)}, u32[]{:S(2)}) %all-to-all-start.3) | async-done | bytes 327712 | tf_op jit(solution)/shard_map/all_to_all | solution.py:19
  202.6 4.7 %all-to-all-start.8 = ((bf16[2,72,512]{2,1,0:T(8,128)(2,1)}), bf16[2,72,512]{2,1,0:T(8,128)(2,1)}, u32[]{:S(2)}, u32[]{:S(2)}) async-start(bf16[2,72,512]{2,1,0:T(8,128)(2,1)} %bitcast.14), calls=%async_computation.8 | async-start | bytes 294912 | tf_op jit(solution)/shard_map/all_to_all | solution.py:19
  207.2 1.6 fusion.1
  208.9 1.9 reshape.159
  210.8 1.2 reduce_sum.104
  212.0 3.2 all-to-all-done.8
  216.4 5.8 %collective-permute-start.6 = (bf16[144,512]{1,0:T(8,128)(2,1)S(1)}, bf16[144,512]{1,0:T(8,128)(2,1)S(1)}, u32[]{:S(2)}, u32[]{:S(2)}) collective-permute-start(bf16[144,512]{1,0:T(8,128)(2,1)S(1)} %fusion.2), channel_id=1, source_target_pairs={{0,256},{256,0},{1,257},{257,1},{2,258},{258,2},{3,259},{259,3},{4... | collective-permute-start | bytes 442376 | tf_op jit(solution)/shard_map/ppermute | solution.py:27
  222.2 1.0 collective-permute-done.6
  224.9 4.1 %all-to-all-start.13 = ((bf16[2,72,512]{2,1,0:T(8,128)(2,1)}), bf16[2,72,512]{2,1,0:T(8,128)(2,1)}, u32[]{:S(2)}, u32[]{:S(2)}) async-start(bf16[2,72,512]{2,1,0:T(8,128)(2,1)} %broadcast_in_dim.64), calls=%async_computation.13 | async-start | bytes 294912 | tf_op jit(solution)/shard_map/all_to_all | solution.py:19
  229.9 1.6 reshape.147
  231.5 5.3 %all-to-all-done.13 = bf16[2,72,512]{2,1,0:T(8,128)(2,1)} async-done(((bf16[2,72,512]{2,1,0:T(8,128)(2,1)}), bf16[2,72,512]{2,1,0:T(8,128)(2,1)}, u32[]{:S(2)}, u32[]{:S(2)}) %all-to-all-start.13) | async-done | bytes 147488 | tf_op jit(solution)/shard_map/all_to_all | solution.py:19
  236.7 1.0 broadcast_in_dim.62
  237.8 20.2 %all_to_all.86 = bf16[64,5,4,128]{3,2,1,0:T(4,128)(2,1)} all-to-all(bf16[64,5,4,128]{3,2,1,0:T(4,128)(2,1)S(1)} %bitcast.58), channel_id=1, replica_groups=mesh['pipe'=2,'x'=4,'yh'=2,'yl'=4,'z'=8] {'yh','yl','z'}, dimensions={0} | all-to-all | bytes 655360 | tf_op jit(solution)/shard_map/all_to_all | solution.py:19
  258.0 1.8 broadcast_in_dim.65
  259.7 4.2 %all-to-all-start.14 = ((bf16[4,2,72,512]{3,2,1,0:T(8,128)(2,1)}), bf16[4,2,72,512]{3,2,1,0:T(8,128)(2,1)}, u32[]{:S(2)}, u32[]{:S(2)}) async-start(bf16[4,2,72,512]{3,2,1,0:T(8,128)(2,1)} %broadcast_in_dim.65), calls=%async_computation.14 | async-start | bytes 1179648 | tf_op jit(solution)/shard_map/all_to_all | solution.py:19
  263.9 1.8 reshape.149
  265.7 5.5 %all-to-all-done.14 = bf16[4,2,72,512]{3,2,1,0:T(8,128)(2,1)} async-done(((bf16[4,2,72,512]{3,2,1,0:T(8,128)(2,1)}), bf16[4,2,72,512]{3,2,1,0:T(8,128)(2,1)}, u32[]{:S(2)}, u32[]{:S(2)}) %all-to-all-start.14) | async-done | bytes 589856 | tf_op jit(solution)/shard_map/all_to_all | solution.py:19
  271.3 2.2 broadcast_in_dim.63
  273.5 4.3 %all-to-all-start.10 = ((bf16[4,2,160,512]{3,2,1,0:T(8,128)(2,1)}), bf16[4,2,160,512]{3,2,1,0:T(8,128)(2,1)}, u32[]{:S(2)}, u32[]{:S(2)}) async-start(bf16[4,2,160,512]{3,2,1,0:T(8,128)(2,1)} %broadcast_in_dim.63), calls=%async_computation.10 | async-start | bytes 2621440 | tf_op jit(solution)/shard_map/all_to_all | solution.py:19
  277.8 3.1 shared.3
  281.7 9.8 %all-to-all-done.10 = bf16[4,2,160,512]{3,2,1,0:T(8,128)(2,1)} async-done(((bf16[4,2,160,512]{3,2,1,0:T(8,128)(2,1)}), bf16[4,2,160,512]{3,2,1,0:T(8,128)(2,1)}, u32[]{:S(2)}, u32[]{:S(2)}) %all-to-all-start.10) | async-done | bytes 1310752 | tf_op jit(solution)/shard_map/all_to_all | solution.py:19
  291.5 3.5 all-to-all-start.15
  295.0 1.2 copy-done.9
  296.2 1.2 copy-done.11
  297.4 4.3 %expert.3 = bf16[8,160,512]{2,1,0:T(8,128)(2,1)} custom-call(s32[1]{0:T(128)} %bitcast.15.first, bf16[8,160,512]{2,1,0:T(8,128)(2,1)} %bitcast.17.g_ref, f32[8,512]{1,0:T(8,128)S(1)} %get-tuple-element.13.gain_ref, bf16[4096,128]{1,0:T(8,128)(2,1)S(1)} %bitcast.47, bf16[4096,128]{1,0:T(8,128)(2,1)S(1)} %bitcast.50, bf16[128,4096]{1,0:T(8,128)(2,1)S(1)} %bitcast.53, ...), custom_call_target="tpu_custom_call" | custom-call | flops 503316480 | bytes 4194304 | tf_op jit(solution)/shard_map/expert/pallas_call | solution.py:105
  302.2 3.7 %all-to-all-start.11 = ((bf16[4,320,512]{2,1,0:T(8,128)(2,1)}), bf16[4,320,512]{2,1,0:T(8,128)(2,1)S(1)}, u32[]{:S(2)}, u32[]{:S(2)}) async-start(bf16[4,320,512]{2,1,0:T(8,128)(2,1)} %bitcast.18), calls=%async_computation.11 | async-start | bytes 2621440 | tf_op jit(solution)/shard_map/all_to_all | solution.py:19
  306.7 10.4 %all-to-all-done.11 = bf16[4,320,512]{2,1,0:T(8,128)(2,1)S(1)} async-done(((bf16[4,320,512]{2,1,0:T(8,128)(2,1)}), bf16[4,320,512]{2,1,0:T(8,128)(2,1)S(1)}, u32[]{:S(2)}, u32[]{:S(2)}) %all-to-all-start.11) | async-done | bytes 1310752 | tf_op jit(solution)/shard_map/all_to_all | solution.py:19
  317.1 8.2 %all-to-all-start.16 = ((bf16[2,72,512]{2,1,0:T(8,128)(2,1)}), bf16[2,72,512]{2,1,0:T(8,128)(2,1)S(1)}, u32[]{:S(2)}, u32[]{:S(2)}) async-start(bf16[2,72,512]{2,1,0:T(8,128)(2,1)} %bitcast.21), calls=%async_computation.16 | async-start | bytes 294912 | tf_op jit(solution)/shard_map/all_to_all | solution.py:19
  326.5 6.2 %all-to-all-done.16 = bf16[2,72,512]{2,1,0:T(8,128)(2,1)S(1)} async-done(((bf16[2,72,512]{2,1,0:T(8,128)(2,1)}), bf16[2,72,512]{2,1,0:T(8,128)(2,1)S(1)}, u32[]{:S(2)}, u32[]{:S(2)}) %all-to-all-start.16) | async-done | bytes 147488 | tf_op jit(solution)/shard_map/all_to_all | solution.py:19
  332.7 8.2 %all-to-all-start.12 = ((bf16[64,5,4,128]{3,2,1,0:T(4,128)(2,1)}), bf16[64,5,4,128]{3,2,1,0:T(4,128)(2,1)S(1)}, u32[]{:S(2)}, u32[]{:S(2)}) async-start(bf16[64,5,4,128]{3,2,1,0:T(4,128)(2,1)} %reshape.152), calls=%async_computation.12 | async-start | bytes 655360 | tf_op jit(solution)/shard_map/all_to_all | solution.py:19
  341.0 12.8 %all-to-all-done.12 = bf16[64,5,4,128]{3,2,1,0:T(4,128)(2,1)S(1)} async-done(((bf16[64,5,4,128]{3,2,1,0:T(4,128)(2,1)}), bf16[64,5,4,128]{3,2,1,0:T(4,128)(2,1)S(1)}, u32[]{:S(2)}, u32[]{:S(2)}) %all-to-all-start.12) | async-done | bytes 327712 | tf_op jit(solution)/shard_map/all_to_all | solution.py:19
  354.2 10.0 %collective-permute-start.7 = (bf16[144,512]{1,0:T(8,128)(2,1)S(1)}, bf16[144,512]{1,0:T(8,128)(2,1)S(1)}, u32[]{:S(2)}, u32[]{:S(2)}) collective-permute-start(bf16[144,512]{1,0:T(8,128)(2,1)S(1)} %fusion.3), channel_id=1, source_target_pairs={{0,256},{256,0},{1,257},{257,1},{2,258},{258,2},{3,259},{259,3},{4... | collective-permute-start | bytes 442376 | tf_op jit(solution)/shard_map/ppermute | solution.py:27
  364.2 1.0 collective-permute-done.7
  (109 shorter events, 17.8 us)
Async XLA Ops:
  6.5 14.1 %copy-start.21 = (s32[1,3,48,8]{2,3,1,0:T(8,128)S(1)}, s32[1,3,48,8]{2,3,1,0:T(8,128)}, u32[]{:S(2)}) copy-start(s32[1,3,48,8]{2,3,1,0:T(8,128)} %param.19) | copy-start | bytes 13828
  6.5 14.2 %copy-start.25 = (s32[1,3,48,8]{2,3,1,0:T(8,128)S(1)}, s32[1,3,48,8]{2,3,1,0:T(8,128)}, u32[]{:S(2)}) copy-start(s32[1,3,48,8]{2,3,1,0:T(8,128)} %param.20) | copy-start | bytes 13828
  6.5 14.6 %copy-start.26 = (f32[1,3,48,8]{2,3,1,0:T(8,128)S(1)}, f32[1,3,48,8]{2,3,1,0:T(8,128)}, u32[]{:S(2)}) copy-start(f32[1,3,48,8]{2,3,1,0:T(8,128)} %param.21) | copy-start | bytes 13828
  6.5 76.9 %all-gather.3.cloned.1.call-start = ((), (), s32[]{:S(2)}) async-start(), calls=%async_computation.17 | async-start | bytes 3538944 | tf_op jit(solution)/shard_map/all_gather | solution.py:145
  7.4 24.0 %copy-start.14 = (bf16[3,48,512]{2,1,0:T(8,128)(2,1)S(1)}, bf16[3,48,512]{2,1,0:T(8,128)(2,1)}, u32[]{:S(2)}) copy-start(bf16[3,48,512]{2,1,0:T(8,128)(2,1)} %param.11) | copy-start | bytes 442372
  21.2 8.5 %collective-permute-start = (f32[144,16]{0,1:T(8,128)S(1)}, f32[144,16]{0,1:T(8,128)S(1)}, u32[]{:S(2)}, u32[]{:S(2)}) collective-permute-start(f32[144,16]{0,1:T(8,128)S(1)} %pad_maximum_fusion.1), channel_id=1, source_target_pairs={{0,256},{256,0},{1,257},{257,1},{2,258},{258,2},{3,259},{259,3},{4... | collective-permute-start | bytes 27656 | tf_op jit(solution)/shard_map/ppermute | solution.py:27
  30.5 2.0 copy-start.15
  32.5 53.7 %all-to-all-start = ((bf16[64,5,4,128]{3,2,1,0:T(4,128)(2,1)}), bf16[64,5,4,128]{3,2,1,0:T(4,128)(2,1)S(1)}, u32[]{:S(2)}, u32[]{:S(2)}) async-start(bf16[64,5,4,128]{3,2,1,0:T(4,128)(2,1)} %bitcast.2), calls=%async_computation | async-start | bytes 655360 | tf_op jit(solution)/shard_map/all_to_all | solution.py:19
  83.5 66.3 %collective-permute-start.5 = (bf16[8,4,128,384]{3,2,1,0:T(8,128)(2,1)}, bf16[8,4,128,384]{3,2,1,0:T(8,128)(2,1)}, u32[]{:S(2)}, u32[]{:S(2)}) collective-permute-start(bf16[8,4,128,384]{3,2,1,0:T(8,128)(2,1)} %bitcast.40), channel_id=1, source_target_pairs={{0,256},{256,0},{1,257},{257,1},{2,258},{258,2},{3,259},{259,3},{4... | collective-permute-start | bytes 9437192 | tf_op jit(solution)/shard_map/ppermute | solution.py:27
  86.9 14.1 %all-to-all-start.4 = ((bf16[2,72,512]{2,1,0:T(8,128)(2,1)}), bf16[2,72,512]{2,1,0:T(8,128)(2,1)S(1)}, u32[]{:S(2)}, u32[]{:S(2)}) async-start(bf16[2,72,512]{2,1,0:T(8,128)(2,1)} %broadcast_in_dim.58), calls=%async_computation.4 | async-start | bytes 294912 | tf_op jit(solution)/shard_map/all_to_all | solution.py:19
  101.0 1.2 copy-start.17
  102.2 4.1 %copy-start.4 = (bf16[1,1,4096,128]{3,2,1,0:T(8,128)(2,1)S(1)}, bf16[1,1,4096,128]{3,2,1,0:T(8,128)(2,1)}, u32[]{:S(2)}) copy-start(bf16[1,1,4096,128]{3,2,1,0:T(8,128)(2,1)} %param.16) | copy-start | bytes 3145732
  102.2 7.6 %copy-start.7 = (bf16[1,1,4096,128]{3,2,1,0:T(8,128)(2,1)S(1)}, bf16[1,1,4096,128]{3,2,1,0:T(8,128)(2,1)}, u32[]{:S(2)}) copy-start(bf16[1,1,4096,128]{3,2,1,0:T(8,128)(2,1)} %param.17) | copy-start | bytes 3145732
  102.2 20.7 %all-to-all-start.1 = ((bf16[4,2,160,512]{3,2,1,0:T(8,128)(2,1)}), bf16[4,2,160,512]{3,2,1,0:T(8,128)(2,1)S(1)}, u32[]{:S(2)}, u32[]{:S(2)}) async-start(bf16[4,2,160,512]{3,2,1,0:T(8,128)(2,1)} %broadcast_in_dim.57), calls=%async_computation.1 | async-start | bytes 2621440 | tf_op jit(solution)/shard_map/all_to_all | solution.py:19
  106.3 23.2 %copy-start.24 = (f32[1,4096]{1,0:T(1,128)S(1)}, f32[1,4096]{1,0:T(1,128)}, u32[]{:S(2)}) copy-start(f32[1,4096]{1,0:T(1,128)} %param.12) | copy-start | bytes 49156
  106.3 29.8 %collective-permute-start.2 = (bf16[4096,128]{1,0:T(8,128)(2,1)S(1)}, bf16[4096,128]{1,0:T(8,128)(2,1)}, u32[]{:S(2)}, u32[]{:S(2)}) collective-permute-start(bf16[4096,128]{1,0:T(8,128)(2,1)S(1)} %bitcast.45), channel_id=1, source_target_pairs={{0,256},{256,0},{1,257},{257,1},{2,258},{258,2},{3,259},{259,3},{4... | collective-permute-start | bytes 3145736 | tf_op jit(solution)/shard_map/ppermute | solution.py:27
  109.8 26.3 %collective-permute-start.3 = (bf16[4096,128]{1,0:T(8,128)(2,1)S(1)}, bf16[4096,128]{1,0:T(8,128)(2,1)}, u32[]{:S(2)}, u32[]{:S(2)}) collective-permute-start(bf16[4096,128]{1,0:T(8,128)(2,1)S(1)} %bitcast.48), channel_id=1, source_target_pairs={{0,256},{256,0},{1,257},{257,1},{2,258},{258,2},{3,259},{259,3},{4... | collective-permute-start | bytes 3145736 | tf_op jit(solution)/shard_map/ppermute | solution.py:27
  111.7 24.4 %collective-permute-start.4 = (bf16[128,4096]{1,0:T(8,128)(2,1)}, bf16[128,4096]{1,0:T(8,128)(2,1)}, u32[]{:S(2)}, u32[]{:S(2)}) collective-permute-start(bf16[128,4096]{1,0:T(8,128)(2,1)} %bitcast.51), channel_id=1, source_target_pairs={{0,256},{256,0},{1,257},{257,1},{2,258},{258,2},{3,259},{259,3},{4... | collective-permute-start | bytes 3145736 | tf_op jit(solution)/shard_map/ppermute | solution.py:27
  122.9 13.2 %copy-start.1 = (bf16[4,2,160,512]{3,2,1,0:T(8,128)(2,1)}, bf16[4,2,160,512]{3,2,1,0:T(8,128)(2,1)S(1)}, u32[]{:S(2)}) copy-start(bf16[4,2,160,512]{3,2,1,0:T(8,128)(2,1)S(1)} %all-to-all-done.1) | copy-start | bytes 3932164
  124.8 20.5 %all-to-all-start.5 = ((bf16[4,2,72,512]{3,2,1,0:T(8,128)(2,1)}), bf16[4,2,72,512]{3,2,1,0:T(8,128)(2,1)}, u32[]{:S(2)}, u32[]{:S(2)}) async-start(bf16[4,2,72,512]{3,2,1,0:T(8,128)(2,1)} %broadcast_in_dim.59), calls=%async_computation.5 | async-start | bytes 1179648 | tf_op jit(solution)/shard_map/all_to_all | solution.py:19
  130.2 4.2 %copy-start.20 = (f32[8,512]{1,0:T(8,128)}, f32[8,512]{1,0:T(8,128)S(1)}, u32[]{:S(2)}) copy-start(f32[8,512]{1,0:T(8,128)S(1)} %reshape_squeeze.3) | copy-start | bytes 49156
  130.2 5.2 %collective-permute-start.1 = (f32[8,512]{1,0:T(8,128)S(1)}, f32[8,512]{1,0:T(8,128)}, u32[]{:S(2)}, u32[]{:S(2)}) collective-permute-start(f32[8,512]{1,0:T(8,128)S(1)} %reshape_squeeze.3), channel_id=1, source_target_pairs={{0,256},{256,0},{1,257},{257,1},{2,258},{258,2},{3,259},{259,3},{4... | collective-permute-start | bytes 49160 | tf_op jit(solution)/shard_map/ppermute | solution.py:27
  136.1 1.3 copy-start.2
  137.4 1.2 copy-start.5
  138.7 1.2 copy-start.8
  139.9 1.2 copy-start.10
  141.1 8.7 %copy-start = (bf16[32,128,384]{2,1,0:T(8,128)(2,1)S(1)}, bf16[32,128,384]{2,1,0:T(8,128)(2,1)}, u32[]{:S(2)}) copy-start(bf16[32,128,384]{2,1,0:T(8,128)(2,1)} %all-gather.3.cloned.1.call-done) | copy-start | bytes 9437188
  144.2 1.1 copy-start.3
  145.3 22.9 %all-to-all-start.2 = ((bf16[4,320,512]{2,1,0:T(8,128)(2,1)}), bf16[4,320,512]{2,1,0:T(8,128)(2,1)}, u32[]{:S(2)}, u32[]{:S(2)}) async-start(bf16[4,320,512]{2,1,0:T(8,128)(2,1)} %bitcast.44), calls=%async_computation.2 | async-start | bytes 2621440 | tf_op jit(solution)/shard_map/all_to_all | solution.py:19
  154.3 0.9 copy-start.13
  168.2 14.1 %all-to-all-start.7 = ((bf16[4,144,512]{2,1,0:T(8,128)(2,1)}), bf16[4,144,512]{2,1,0:T(8,128)(2,1)}, u32[]{:S(2)}, u32[]{:S(2)}) async-start(bf16[4,144,512]{2,1,0:T(8,128)(2,1)} %bitcast.55), calls=%async_computation.7 | async-start | bytes 1179648 | tf_op jit(solution)/shard_map/all_to_all | solution.py:19
  172.4 17.2 %copy-start.23 = (f32[144,8]{0,1:T(8,128)S(1)}, f32[144,8]{0,1:T(8,128)}, u32[]{:S(2)}) copy-start(f32[144,8]{0,1:T(8,128)} %get-tuple-element.18) | copy-start | bytes 13828
  172.4 17.3 %copy-start.22 = (f32[144,8]{0,1:T(8,128)S(1)}, f32[144,8]{0,1:T(8,128)}, u32[]{:S(2)}) copy-start(f32[144,8]{0,1:T(8,128)} %get-tuple-element.21) | copy-start | bytes 13828
  174.7 32.5 %copy-start.16 = (f32[144,8]{1,0:T(8,128)S(1)}, f32[144,8]{1,0:T(8,128)}, u32[]{:S(2)}) copy-start(f32[144,8]{1,0:T(8,128)} %copy-done.15) | copy-start | bytes 13828
  182.3 20.3 %all-to-all-start.3 = ((bf16[64,5,4,128]{3,2,1,0:T(4,128)(2,1)}), bf16[64,5,4,128]{3,2,1,0:T(4,128)(2,1)}, u32[]{:S(2)}, u32[]{:S(2)}) async-start(bf16[64,5,4,128]{3,2,1,0:T(4,128)(2,1)} %reshape.141), calls=%async_computation.3 | async-start | bytes 655360 | tf_op jit(solution)/shard_map/all_to_all | solution.py:19
  202.6 12.6 %all-to-all-start.8 = ((bf16[2,72,512]{2,1,0:T(8,128)(2,1)}), bf16[2,72,512]{2,1,0:T(8,128)(2,1)}, u32[]{:S(2)}, u32[]{:S(2)}) async-start(bf16[2,72,512]{2,1,0:T(8,128)(2,1)} %bitcast.14), calls=%async_computation.8 | async-start | bytes 294912 | tf_op jit(solution)/shard_map/all_to_all | solution.py:19
  208.9 7.3 %copy-start.19 = (bf16[160,144]{0,1:T(8,128)(2,1)S(1)}, bf16[160,144]{0,1:T(8,128)(2,1)}, u32[]{:S(2)}) copy-start(bf16[160,144]{0,1:T(8,128)(2,1)} %get-tuple-element.8) | copy-start | bytes 138244
  216.4 6.8 %collective-permute-start.6 = (bf16[144,512]{1,0:T(8,128)(2,1)S(1)}, bf16[144,512]{1,0:T(8,128)(2,1)S(1)}, u32[]{:S(2)}, u32[]{:S(2)}) collective-permute-start(bf16[144,512]{1,0:T(8,128)(2,1)S(1)} %fusion.2), channel_id=1, source_target_pairs={{0,256},{256,0},{1,257},{257,1},{2,258},{258,2},{3,259},{259,3},{4... | collective-permute-start | bytes 442376 | tf_op jit(solution)/shard_map/ppermute | solution.py:27
  224.9 11.9 %all-to-all-start.13 = ((bf16[2,72,512]{2,1,0:T(8,128)(2,1)}), bf16[2,72,512]{2,1,0:T(8,128)(2,1)}, u32[]{:S(2)}, u32[]{:S(2)}) async-start(bf16[2,72,512]{2,1,0:T(8,128)(2,1)} %broadcast_in_dim.64), calls=%async_computation.13 | async-start | bytes 294912 | tf_op jit(solution)/shard_map/all_to_all | solution.py:19
  259.7 11.5 %all-to-all-start.14 = ((bf16[4,2,72,512]{3,2,1,0:T(8,128)(2,1)}), bf16[4,2,72,512]{3,2,1,0:T(8,128)(2,1)}, u32[]{:S(2)}, u32[]{:S(2)}) async-start(bf16[4,2,72,512]{3,2,1,0:T(8,128)(2,1)} %broadcast_in_dim.65), calls=%async_computation.14 | async-start | bytes 1179648 | tf_op jit(solution)/shard_map/all_to_all | solution.py:19
  273.5 18.0 %all-to-all-start.10 = ((bf16[4,2,160,512]{3,2,1,0:T(8,128)(2,1)}), bf16[4,2,160,512]{3,2,1,0:T(8,128)(2,1)}, u32[]{:S(2)}, u32[]{:S(2)}) async-start(bf16[4,2,160,512]{3,2,1,0:T(8,128)(2,1)} %broadcast_in_dim.63), calls=%async_computation.10 | async-start | bytes 2621440 | tf_op jit(solution)/shard_map/all_to_all | solution.py:19
  280.8 0.8 copy-start.12
  281.6 13.3 %copy-start.6 = (bf16[1,1,4096,128]{3,2,1,0:T(8,128)(2,1)S(1)}, bf16[1,1,4096,128]{3,2,1,0:T(8,128)(2,1)}, u32[]{:S(2)}) copy-start(bf16[1,1,4096,128]{3,2,1,0:T(8,128)(2,1)} %param.16) | copy-start | bytes 3145732
  291.5 10.7 %all-to-all-start.15 = ((bf16[4,144,512]{2,1,0:T(8,128)(2,1)}), bf16[4,144,512]{2,1,0:T(8,128)(2,1)S(1)}, u32[]{:S(2)}, u32[]{:S(2)}) async-start(bf16[4,144,512]{2,1,0:T(8,128)(2,1)} %bitcast.54), calls=%async_computation.15 | async-start | bytes 1179648 | tf_op jit(solution)/shard_map/all_to_all | solution.py:19
  295.0 1.2 copy-start.9
  296.2 1.2 copy-start.11
  302.2 14.9 %all-to-all-start.11 = ((bf16[4,320,512]{2,1,0:T(8,128)(2,1)}), bf16[4,320,512]{2,1,0:T(8,128)(2,1)S(1)}, u32[]{:S(2)}, u32[]{:S(2)}) async-start(bf16[4,320,512]{2,1,0:T(8,128)(2,1)} %bitcast.18), calls=%async_computation.11 | async-start | bytes 2621440 | tf_op jit(solution)/shard_map/all_to_all | solution.py:19
  317.1 15.5 %all-to-all-start.16 = ((bf16[2,72,512]{2,1,0:T(8,128)(2,1)}), bf16[2,72,512]{2,1,0:T(8,128)(2,1)S(1)}, u32[]{:S(2)}, u32[]{:S(2)}) async-start(bf16[2,72,512]{2,1,0:T(8,128)(2,1)} %bitcast.21), calls=%async_computation.16 | async-start | bytes 294912 | tf_op jit(solution)/shard_map/all_to_all | solution.py:19
  332.7 21.1 %all-to-all-start.12 = ((bf16[64,5,4,128]{3,2,1,0:T(4,128)(2,1)}), bf16[64,5,4,128]{3,2,1,0:T(4,128)(2,1)S(1)}, u32[]{:S(2)}, u32[]{:S(2)}) async-start(bf16[64,5,4,128]{3,2,1,0:T(4,128)(2,1)} %reshape.152), calls=%async_computation.12 | async-start | bytes 655360 | tf_op jit(solution)/shard_map/all_to_all | solution.py:19
  341.0 13.0 %copy-start.18 = (bf16[160,144]{0,1:T(8,128)(2,1)S(1)}, bf16[160,144]{0,1:T(8,128)(2,1)}, u32[]{:S(2)}) copy-start(bf16[160,144]{0,1:T(8,128)(2,1)} %get-tuple-element.7) | copy-start | bytes 138244
  354.2 11.0 %collective-permute-start.7 = (bf16[144,512]{1,0:T(8,128)(2,1)S(1)}, bf16[144,512]{1,0:T(8,128)(2,1)S(1)}, u32[]{:S(2)}, u32[]{:S(2)}) collective-permute-start(bf16[144,512]{1,0:T(8,128)(2,1)S(1)} %fusion.3), channel_id=1, source_target_pairs={{0,256},{256,0},{1,257},{257,1},{2,258},{258,2},{3,259},{259,3},{4... | collective-permute-start | bytes 442376 | tf_op jit(solution)/shard_map/ppermute | solution.py:27
Sparse Core Ops, SparseCore 0:
  20.8 62.6 all-gather.2
